TPU v7x, 128 devices: a whole 4x4x4 slice. The times are simulated.
128 devices in a mesh: don: 8 (over x, core), acc: 16 (over y, z).
Axes of the slice: x: 4, y: 4, z: 4, core: 2. Of those that a mesh axis runs over, the one named last changes fastest.
Arguments:
- donor_emb: bfloat16 [262144, 768], P(('don', 'acc')), may hold values from -12 to 12
- acceptor_emb: bfloat16 [262144, 768], P(('don', 'acc')), may hold values from -6 to 6
- donor_pos: int32 [3072], P(('don', 'acc')), may hold values from 0 to 2047
- acceptor_pos: int32 [3072], P(('don', 'acc')), may hold values from 0 to 2047
- donor_count: int32 [128], P('don'), may hold values from 1 to 24, as said below
- acceptor_count: int32 [128], replicated, may hold values from 1 to 24, as said below
- target: int32 [64, 3072], P(None, 'don'), may hold values from 0 to 3071, as said below
- junction_mask: int32 [64, 3072], P(None, 'don'), may hold values 0 or 1
- weights: bfloat16 [64, 768, 768], P('acc'), may hold values from -1 to 2
Outputs:
- loss: float32 [], replicated
- grad_weight: float32 [768, 64, 768], P('don', 'acc')
Inputs may be any that keep to these rules, and one draw needn't show every extreme that they name: `donor_count`: the live donor slots of all shards number exactly 1600; some shard has all 24 live. `acceptor_count`: the live acceptor slots of all shards number exactly 1600; some shard has all 24 live. `target`: each entry names a live acceptor slot.
All inputs are finite; a program needn't handle non-finite values. No bound on the sum of `junction_mask` on one device may be relied on, other than what follows from the above.
Results may differ from a plain program's by a relative error of at most 0.0031.
Values may be sent and summed in bfloat16 or wider, within the bound.
No kernel may reach another device: no remote copies, remote signals or barrier semaphores. Data moves between devices by JAX's collectives and lax.ppermute only.
A program may use at most 128 MiB of HBM per device.

v0:
```python
import jax
import jax.numpy as jnp
from jax import lax
from jax.sharding import Mesh
from jax.sharding import PartitionSpec as P

ACC = ("acc_0", "acc_1")
DON = ("don_0", "don_1")
DON_ACC = ("don_0", "don_1", "acc_0", "acc_1")


def one_axis_at_a_time(shard, axes):
    for axis in axes:
        shard = lax.psum(shard, axis)
    return shard


def local(
    donor_emb,
    acceptor_emb,
    donor_pos,
    acceptor_pos,
    donor_count,
    acceptor_count,
    target,
    junction_mask,
    weights,
):
    slots = donor_pos.shape[0]
    width = weights.shape[1]
    tis_dev = weights.shape[0]
    scale = width ** (-0.5)
    column = lax.axis_index(ACC)
    donor_local = jnp.take(donor_emb, donor_pos, axis=0)
    acceptor_local = jnp.take(acceptor_emb, acceptor_pos, axis=0)
    donors = lax.all_gather(donor_local, ACC, axis=0, tiled=True)
    acceptors = lax.all_gather(acceptor_local, DON_ACC, axis=0, tiled=True)
    donor_rows = donors.shape[0]
    acceptor_rows = acceptors.shape[0]
    live_d = jnp.arange(donor_rows, dtype=jnp.int32) % slots < jnp.repeat(donor_count, slots)
    live_a = jnp.arange(acceptor_rows, dtype=jnp.int32) % slots < jnp.repeat(acceptor_count, slots)
    first_tissue = column * tis_dev
    targets_dev = lax.dynamic_slice_in_dim(target, first_tissue, tis_dev, 0)
    masks_dev = lax.dynamic_slice_in_dim(junction_mask, first_tissue, tis_dev, 0)
    weighting = jnp.where(live_d[None, :], masks_dev, 0).astype(jnp.float32)
    columns = jnp.arange(acceptor_rows, dtype=jnp.int32)

    def tissue(inputs):
        matrix, target_row, weight_row = inputs
        projected = jnp.dot(donors, matrix, preferred_element_type=jnp.float32).astype(jnp.bfloat16)
        scores = (
            lax.dot_general(
                projected, acceptors, (((1,), (1,)), ((), ())), preferred_element_type=jnp.float32
            )
            * scale
        )
        scores = jnp.where(live_a[None, :], scores, -1e30)
        highest = jnp.max(scores, axis=1, keepdims=True)
        summed_exp = jnp.sum(
            jnp.where(live_a[None, :], jnp.exp(scores - highest), 0.0), axis=1, keepdims=True
        )
        log_total = highest + jnp.log(summed_exp)
        is_target = columns[None, :] == target_row[:, None]
        picked = jnp.sum(jnp.where(is_target, scores, 0.0), axis=1)
        summed = jnp.sum(weight_row * (log_total[:, 0] - picked))
        counted = jnp.sum(weight_row)
        probs = jnp.where(live_a[None, :], jnp.exp(scores - log_total), 0.0)
        dscore = (weight_row[:, None] * (probs - is_target.astype(jnp.float32))).astype(
            jnp.bfloat16
        )
        dproj = (jnp.dot(dscore, acceptors, preferred_element_type=jnp.float32) * scale).astype(
            jnp.bfloat16
        )
        return (summed, counted, dproj)

    summed, counted, dproj = lax.map(tissue, (weights, targets_dev, weighting))
    summed, counted = (
        one_axis_at_a_time(jnp.sum(summed), DON_ACC),
        one_axis_at_a_time(jnp.sum(counted), DON_ACC),
    )
    loss = summed / jnp.maximum(counted, 1.0)
    grad_weight = lax.psum_scatter(
        jnp.einsum("nd,tne->dte", donors, dproj, preferred_element_type=jnp.float32),
        DON,
        scatter_dimension=0,
        tiled=True,
    )
    return (loss, grad_weight)


def solution(mesh):
    finer = Mesh(mesh.devices.reshape(4, 2, 4, 4), ("don_0", "don_1", "acc_0", "acc_1"))
    return jax.shard_map(
        local,
        mesh=finer,
        in_specs=(
            P(DON_ACC, None),
            P(DON_ACC, None),
            P(DON_ACC),
            P(DON_ACC),
            P(DON),
            P(),
            P(None, DON),
            P(None, DON),
            P(ACC, None, None),
        ),
        out_specs=(P(), P(DON, ACC, None)),
        check_vma=False,
    )
```

profile of v0, /device:TPU:1, one launch (start us, length us, event | category | flops | bytes accessed | tf_op | source)
XLA Modules:
  0.0 247.4 jit_solution(5175698280797513508)
XLA Ops:
  7.2 0.8 compare_select_fusion
  11.3 2.9 %gather_fusion = bf16[24,768]{1,0:T(8,128)(2,1)S(1)} fusion(bf16[2048,768]{1,0:T(8,128)(2,1)} %param.13, s32[1024]{0:T(1024)S(1)} %pad_clamp_fusion.1), kind=kCustom, calls=%fused_computation.clone | custom fusion | bytes 73824 | tf_op jit(solution)/shard_map/jit(_take)/gather | solution.py:34
  14.3 23.8 %all_gather.6 = bf16[384,768]{1,0:T(8,128)(2,1)} all-gather(bf16[24,768]{1,0:T(8,128)(2,1)S(1)} %broadcast_select_fusion.1), channel_id=1, replica_groups=mesh['don_0'=4,'don_1'=2,'acc_0'=4,'acc_1'=4] {'acc_0','acc_1'}, dimensions={0}, use_global_device_ids=true | all-gather | bytes 626688 | tf_op jit(solution)/shard_map/all_gather | solution.py:36
  38.9 43.2 %all-gather.2.cloned.1.call-done = bf16[3072,768]{1,0:T(8,128)(2,1)} async-done(((bf16[24,768]{1,0:T(8,128)(2,1)}), bf16[3072,768]{1,0:T(8,128)(2,1)}) %all-gather.2.cloned.1.call-update) | async-done | bytes 4718608 | tf_op jit(solution)/shard_map/all_gather | solution.py:37
  82.1 91.8 %while.15 = (s32[]{:T(128)}, f32[4]{0:T(128)S(1)}, f32[4]{0:T(128)S(1)}, bf16[4,384,768]{2,1,0:T(8,128)(2,1)}, f32[4,384]{1,0:T(4,128)S(1)}, /*index=5*/bf16[4,7...) while((s32[]{:T(128)}, f32[4]{0:T(128)S(1)}, ...), condition=%wide.region_6.8_spmd.clone, body=%wide.region_0.7_spmd.clone.sunk | while | flops 4096644864 | bytes 26040484 | solution.py:76
  83.5 7.9 %fusion.72 = (f32[384]{0:T(512)S(1)}, f32[384,3072]{1,0:T(8,128)}) fusion(bf16[3072,768]{1,0:T(8,128)(2,1)} %get-tuple-element.241, bf16[384,768]{1,0:T(8,128)(2,1)} %get-tuple-element.240, bf16[4,768,768]{2,1,0:T(8,128)(2,1)} %get-tuple-element.239, s32[]{:T(128)S(6)} %copy.20, pred[3072]{0:T(1024)(128)(4,1)S(1)} %fusion.71), kind=kOutput, calls=%fused_computation.58.clone.1 | convolution fusion | flops 2268757504 | bytes 11211268 | tf_op jit(solution)/shard_map/while/body/eval_jaxpr/dot_general | solution.py:52
  91.4 4.0 %fusion.73 = (f32[384]{0:T(512)S(1)}, f32[384]{0:T(512)S(1)}) fusion(f32[384,3072]{1,0:T(8,128)} %get-tuple-element.205, s32[384]{0:T(512)S(1)} %dynamic-slice_reduce_fusion.2, f32[384]{0:T(512)S(1)} %get-tuple-element.206, pred[3072]{0:T(1024)(128)(4,1)S(1)} %fusion.71), kind=kLoop, calls=%fused_computation.7.clone.1 | loop fusion | flops 7077120 | bytes 4727808 | tf_op jit(solution)/shard_map/while/body/eval_jaxpr/reduce_sum | solution.py:64
  97.6 7.4 %fusion.74 = bf16[4,384,768]{2,1,0:T(8,128)(2,1)} fusion(bf16[4,384,768]{2,1,0:T(8,128)(2,1)} %get-tuple-element.226, s32[]{:T(128)S(6)} %copy.20, bf16[3072,768]{1,0:T(8,128)(2,1)} %get-tuple-element.241, f32[384,3072]{1,0:T(8,128)} %get-tuple-element.205, f32[384]{0:T(512)S(1)} %get-tuple-element.211, f32[384]{0:T(512)S(1)} %get-tuple-element.204, ...), kind=kOutput, calls=%fused_computation.23.clone.1 | convolution fusion | flops 1820786688 | bytes 10034692 | tf_op jit(solution)/shard_map/while/body/eval_jaxpr/dot_general | solution.py:71
  106.5 7.9 %fusion.72 = (f32[384]{0:T(512)S(1)}, f32[384,3072]{1,0:T(8,128)}) fusion(bf16[3072,768]{1,0:T(8,128)(2,1)} %get-tuple-element.241, bf16[384,768]{1,0:T(8,128)(2,1)} %get-tuple-element.240, bf16[4,768,768]{2,1,0:T(8,128)(2,1)} %get-tuple-element.239, s32[]{:T(128)S(6)} %copy.20, pred[3072]{0:T(1024)(128)(4,1)S(1)} %fusion.71), kind=kOutput, calls=%fused_computation.58.clone.1 | convolution fusion | flops 2268757504 | bytes 11211268 | tf_op jit(solution)/shard_map/while/body/eval_jaxpr/dot_general | solution.py:52
  114.4 4.0 %fusion.73 = (f32[384]{0:T(512)S(1)}, f32[384]{0:T(512)S(1)}) fusion(f32[384,3072]{1,0:T(8,128)} %get-tuple-element.205, s32[384]{0:T(512)S(1)} %dynamic-slice_reduce_fusion.2, f32[384]{0:T(512)S(1)} %get-tuple-element.206, pred[3072]{0:T(1024)(128)(4,1)S(1)} %fusion.71), kind=kLoop, calls=%fused_computation.7.clone.1 | loop fusion | flops 7077120 | bytes 4727808 | tf_op jit(solution)/shard_map/while/body/eval_jaxpr/reduce_sum | solution.py:64
  120.5 7.4 %fusion.74 = bf16[4,384,768]{2,1,0:T(8,128)(2,1)} fusion(bf16[4,384,768]{2,1,0:T(8,128)(2,1)} %get-tuple-element.226, s32[]{:T(128)S(6)} %copy.20, bf16[3072,768]{1,0:T(8,128)(2,1)} %get-tuple-element.241, f32[384,3072]{1,0:T(8,128)} %get-tuple-element.205, f32[384]{0:T(512)S(1)} %get-tuple-element.211, f32[384]{0:T(512)S(1)} %get-tuple-element.204, ...), kind=kOutput, calls=%fused_computation.23.clone.1 | convolution fusion | flops 1820786688 | bytes 10034692 | tf_op jit(solution)/shard_map/while/body/eval_jaxpr/dot_general | solution.py:71
  129.4 7.9 %fusion.72 = (f32[384]{0:T(512)S(1)}, f32[384,3072]{1,0:T(8,128)}) fusion(bf16[3072,768]{1,0:T(8,128)(2,1)} %get-tuple-element.241, bf16[384,768]{1,0:T(8,128)(2,1)} %get-tuple-element.240, bf16[4,768,768]{2,1,0:T(8,128)(2,1)} %get-tuple-element.239, s32[]{:T(128)S(6)} %copy.20, pred[3072]{0:T(1024)(128)(4,1)S(1)} %fusion.71), kind=kOutput, calls=%fused_computation.58.clone.1 | convolution fusion | flops 2268757504 | bytes 11211268 | tf_op jit(solution)/shard_map/while/body/eval_jaxpr/dot_general | solution.py:52
  137.3 4.0 %fusion.73 = (f32[384]{0:T(512)S(1)}, f32[384]{0:T(512)S(1)}) fusion(f32[384,3072]{1,0:T(8,128)} %get-tuple-element.205, s32[384]{0:T(512)S(1)} %dynamic-slice_reduce_fusion.2, f32[384]{0:T(512)S(1)} %get-tuple-element.206, pred[3072]{0:T(1024)(128)(4,1)S(1)} %fusion.71), kind=kLoop, calls=%fused_computation.7.clone.1 | loop fusion | flops 7077120 | bytes 4727808 | tf_op jit(solution)/shard_map/while/body/eval_jaxpr/reduce_sum | solution.py:64
  143.5 7.5 %fusion.74 = bf16[4,384,768]{2,1,0:T(8,128)(2,1)} fusion(bf16[4,384,768]{2,1,0:T(8,128)(2,1)} %get-tuple-element.226, s32[]{:T(128)S(6)} %copy.20, bf16[3072,768]{1,0:T(8,128)(2,1)} %get-tuple-element.241, f32[384,3072]{1,0:T(8,128)} %get-tuple-element.205, f32[384]{0:T(512)S(1)} %get-tuple-element.211, f32[384]{0:T(512)S(1)} %get-tuple-element.204, ...), kind=kOutput, calls=%fused_computation.23.clone.1 | convolution fusion | flops 1820786688 | bytes 10034692 | tf_op jit(solution)/shard_map/while/body/eval_jaxpr/dot_general | solution.py:71
  152.4 7.9 %fusion.72 = (f32[384]{0:T(512)S(1)}, f32[384,3072]{1,0:T(8,128)}) fusion(bf16[3072,768]{1,0:T(8,128)(2,1)} %get-tuple-element.241, bf16[384,768]{1,0:T(8,128)(2,1)} %get-tuple-element.240, bf16[4,768,768]{2,1,0:T(8,128)(2,1)} %get-tuple-element.239, s32[]{:T(128)S(6)} %copy.20, pred[3072]{0:T(1024)(128)(4,1)S(1)} %fusion.71), kind=kOutput, calls=%fused_computation.58.clone.1 | convolution fusion | flops 2268757504 | bytes 11211268 | tf_op jit(solution)/shard_map/while/body/eval_jaxpr/dot_general | solution.py:52
  160.3 4.0 %fusion.73 = (f32[384]{0:T(512)S(1)}, f32[384]{0:T(512)S(1)}) fusion(f32[384,3072]{1,0:T(8,128)} %get-tuple-element.205, s32[384]{0:T(512)S(1)} %dynamic-slice_reduce_fusion.2, f32[384]{0:T(512)S(1)} %get-tuple-element.206, pred[3072]{0:T(1024)(128)(4,1)S(1)} %fusion.71), kind=kLoop, calls=%fused_computation.7.clone.1 | loop fusion | flops 7077120 | bytes 4727808 | tf_op jit(solution)/shard_map/while/body/eval_jaxpr/reduce_sum | solution.py:64
  166.5 7.4 %fusion.74 = bf16[4,384,768]{2,1,0:T(8,128)(2,1)} fusion(bf16[4,384,768]{2,1,0:T(8,128)(2,1)} %get-tuple-element.226, s32[]{:T(128)S(6)} %copy.20, bf16[3072,768]{1,0:T(8,128)(2,1)} %get-tuple-element.241, f32[384,3072]{1,0:T(8,128)} %get-tuple-element.205, f32[384]{0:T(512)S(1)} %get-tuple-element.211, f32[384]{0:T(512)S(1)} %get-tuple-element.204, ...), kind=kOutput, calls=%fused_computation.23.clone.1 | convolution fusion | flops 1820786688 | bytes 10034692 | tf_op jit(solution)/shard_map/while/body/eval_jaxpr/dot_general | solution.py:71
  173.9 8.1 %fusion.42 = f32[768,4,768]{2,0,1:T(8,128)} fusion(bf16[4,384,768]{2,1,0:T(8,128)(2,1)} %get-tuple-element.64, bf16[384,768]{1,0:T(8,128)(2,1)} %get-tuple-element.249), kind=kOutput, calls=%fused_computation.40 | convolution fusion | flops 1811939328 | bytes 12386304 | tf_op jit(solution)/shard_map/nd,tne->dte/dot_general | solution.py:83
  183.3 7.4 %all-reduce.2 = (f32[]{:T(128)}, f32[]{:T(128)}) all-reduce(f32[]{:T(128)} %reduce_sum.54, f32[]{:T(128)} %reduce_sum.55), channel_id=1, replica_groups=mesh['don_0'=4,'don_1'=2,'acc_0'=4,'acc_1'=4] {'don_0'}, use_global_device_ids=true, to_apply=%region_8.10 | all-reduce | flops 2 | bytes 16 | tf_op jit(solution)/shard_map/psum | solution.py:14
  190.7 5.0 %all-reduce.3 = (f32[]{:T(128)}, f32[]{:T(128)}) all-reduce(f32[]{:T(128)} %get-tuple-element.121, f32[]{:T(128)} %get-tuple-element.122), channel_id=1, replica_groups=mesh['don_0'=4,'don_1'=2,'acc_0'=4,'acc_1'=4] {'don_1'}, use_global_device_ids=true, to_apply=%region_9.11 | all-reduce | flops 2 | bytes 16 | tf_op jit(solution)/shard_map/psum | solution.py:14
  195.7 9.4 %all-reduce.1 = (f32[]{:T(128)}, f32[]{:T(128)}) all-reduce(f32[]{:T(128)} %get-tuple-element.123, f32[]{:T(128)} %get-tuple-element.124), channel_id=1, replica_groups=mesh['don_0'=4,'don_1'=2,'acc_0'=4,'acc_1'=4] {'acc_0'}, use_global_device_ids=true, to_apply=%region_10.12 | all-reduce | flops 2 | bytes 16 | tf_op jit(solution)/shard_map/psum | solution.py:14
  205.1 8.1 %all-reduce = (f32[]{:T(128)}, f32[]{:T(128)}) all-reduce(f32[]{:T(128)} %get-tuple-element.119, f32[]{:T(128)} %get-tuple-element.120), channel_id=1, replica_groups=mesh['don_0'=4,'don_1'=2,'acc_0'=4,'acc_1'=4] {'acc_1'}, use_global_device_ids=true, to_apply=%region_11.13 | all-reduce | flops 2 | bytes 16 | tf_op jit(solution)/shard_map/psum | solution.py:14
  214.5 21.8 %reduce-scatter.2.cloned.1.call-done = f32[96,4,768]{2,0,1:T(8,128)} async-done(((f32[768,4,768]{2,0,1:T(8,128)}), f32[96,4,768]{2,0,1:T(8,128)}) %reduce-scatter.2.cloned.1.call-update) | async-done | bytes 1179664 | tf_op jit(solution)/shard_map/reduce_scatter | solution.py:82
  236.4 3.0 %copy.12 = f32[96,4,768]{2,1,0:T(4,128)} copy(f32[96,4,768]{2,0,1:T(8,128)} %reduce-scatter.2.cloned.1.call-done) | data formatting | bytes 2359296
  (53 shorter events, 19.9 us)
Async XLA Ops:
  7.2 1.9 copy-start
  7.2 74.9 %all-gather.2.cloned.1.call-start = ((), (), s32[]{:S(2)}) async-start(), calls=%async_computation.1 | async-start | bytes 4755456 | tf_op jit(solution)/shard_map/all_gather | solution.py:37
  10.4 226.0 %reduce-scatter.2.cloned.1.call-start = ((), (), s32[]{:S(2)}) async-start(), calls=%async_computation.2 | async-start | bytes 10616832 | tf_op jit(solution)/shard_map/reduce_scatter | solution.py:82
Sparse Core Ops, SparseCore 0:
  11.7 70.3 all-gather.1
  182.2 54.1 reduce-scatter.1
where the time goes:
time: 248 us; the launch traced here: 247 us
  matrix products  69.4 us (28%)
  waiting for transfers between devices  65 us (26%)
  blocking collectives  53.8 us (22%)
  other arithmetic  25.5 us (10%)
  local copies, waits for them, and re-layouts  17 us (7%)
  between operations  16.5 us (7%)
    all_gather x1, waiting for transfers between devices, local(): acceptors = lax.all_gather(acceptor_local, DON_ACC, axis=0, tiled=True)  43.2 us
    dot_general x4, matrix products, tissue(): lax.dot_general(projected, acceptors, (((1,), (1,)), ((), ())), preferred...  31.5 us
    psum x4, blocking collectives, one_axis_at_a_time(): shard = lax.psum(shard, axis)  30 us
    dot_general x4, matrix products, tissue(): jnp.dot(dscore, acceptors, preferred_element_type=jnp.float32) * scale  29.8 us
    all_gather x1, blocking collectives, local(): donors = lax.all_gather(donor_local, ACC, axis=0, tiled=True)  23.8 us
    reduce_scatter x1, waiting for transfers between devices, local(): lax.psum_scatter(jnp.einsum('nd,tne->dte', donors, dproj, preferred_eleme...  21.8 us
    reduce_sum x4, other arithmetic, tissue(): picked = jnp.sum(jnp.where(is_target, scores, 0.0), axis=1)  16 us
    dot_general x1, matrix products, local(): jnp.einsum('nd,tne->dte', donors, dproj, preferred_element_type=jnp.float32)  8.13 us
  transfers between devices with their start and end apart: 2, of which 2 were waited for; matrix products, arithmetic and copies ran while one was open for 2% of the time, Pallas kernels for 0%

commit v1 on v0

--- a/solution.py
+++ b/solution.py
@@ -11,7 +11,7 @@
 
 def one_axis_at_a_time(shard, axes):
     for axis in axes:
-        shard = lax.psum(shard, axis)
+        shard = jnp.sum(lax.all_gather(shard, axis), axis=0)
     return shard
 
 

time: 248 us -> 243 us (0.980)
  waiting for transfers between devices: 65 us -> 48 us
  local copies, waits for them, and re-layouts: 17 us -> 31.4 us
  other arithmetic: 25.5 us -> 31.2 us
  matrix products: 69.4 us -> 63.9 us
    psum x4 -> x0, blocking collectives: 30 us -> none  [one_axis_at_a_time(): shard = lax.psum(shard, axis)]
    unnamed x0 -> x4, blocking collectives: none -> 27.5 us
    reduce_scatter x1, waiting for transfers between devices: 21.8 us -> 4.83 us  [local(): lax.psum_scatter(jnp.einsum('nd,tne->dte', donors, dproj, preferred_eleme...]
    unnamed x3 -> x33, local copies, waits for them, and re-layouts: 3.31 us -> 17.7 us
    dot_general x4, matrix products: 29.8 us -> 24.2 us  [tissue(): jnp.dot(dscore, acceptors, preferred_element_type=jnp.float32) * scale]
    reduce_sum x0 -> x8, other arithmetic: none -> 5.05 us  [one_axis_at_a_time(): shard = jnp.sum(lax.all_gather(shard, axis), axis=0)]
  transfers between devices with their start and end apart: 2 -> 2, of which waited for: 2 -> 2; matrix products, arithmetic and copies ran while one was open for 2% -> 10% of each run, Pallas kernels for 0% -> 0%
where the time goes in v1:
time: 243 us
  matrix products  63.9 us (26%)
  blocking collectives  51.4 us (21%)
  waiting for transfers between devices  48 us (20%)
  local copies, waits for them, and re-layouts  31.4 us (13%)
  other arithmetic  31.2 us (13%)
  between operations  16.6 us (7%)
    all_gather x1, waiting for transfers between devices, local(): acceptors = lax.all_gather(acceptor_local, DON_ACC, axis=0, tiled=True)  43.2 us
    dot_general x4, matrix products, tissue(): lax.dot_general(projected, acceptors, (((1,), (1,)), ((), ())), preferred...  31.5 us
    unnamed x4, blocking collectives  27.5 us
    dot_general x4, matrix products, tissue(): jnp.dot(dscore, acceptors, preferred_element_type=jnp.float32) * scale  24.2 us
    all_gather x1, blocking collectives, local(): donors = lax.all_gather(donor_local, ACC, axis=0, tiled=True)  23.8 us
    unnamed x33, local copies, waits for them, and re-layouts  17.7 us
    reduce_sum x4, other arithmetic, tissue(): picked = jnp.sum(jnp.where(is_target, scores, 0.0), axis=1)  16.5 us
    dot_general x1, matrix products, local(): jnp.einsum('nd,tne->dte', donors, dproj, preferred_element_type=jnp.float32)  8.13 us
  transfers between devices with their start and end apart: 2, of which 2 were waited for; matrix products, arithmetic and copies ran while one was open for 10% of the time, Pallas kernels for 0%

profile of v1, /device:TPU:1, one launch (start us, length us, event | category | flops | bytes accessed | tf_op | source)
XLA Modules:
  0.0 242.5 jit_solution(16570760462636401974)
XLA Ops:
  11.3 2.9 %gather_fusion = bf16[24,768]{1,0:T(8,128)(2,1)S(1)} fusion(bf16[2048,768]{1,0:T(8,128)(2,1)} %param.13, s32[1024]{0:T(1024)S(1)} %pad_clamp_fusion.1), kind=kCustom, calls=%fused_computation.clone | custom fusion | bytes 73824 | tf_op jit(solution)/shard_map/jit(_take)/gather | solution.py:34
  14.3 23.8 %all_gather.54 = bf16[384,768]{1,0:T(8,128)(2,1)} all-gather(bf16[24,768]{1,0:T(8,128)(2,1)S(1)} %broadcast_select_fusion.1), channel_id=1, replica_groups=mesh['don_0'=4,'don_1'=2,'acc_0'=4,'acc_1'=4] {'acc_0','acc_1'}, dimensions={0}, use_global_device_ids=true | all-gather | bytes 626688 | tf_op jit(solution)/shard_map/all_gather | solution.py:36
  38.9 43.2 %all-gather.2.cloned.1.call-done = bf16[3072,768]{1,0:T(8,128)(2,1)} async-done(((bf16[24,768]{1,0:T(8,128)(2,1)}), bf16[3072,768]{1,0:T(8,128)(2,1)}) %all-gather.2.cloned.1.call-update) | async-done | bytes 4718608 | tf_op jit(solution)/shard_map/all_gather | solution.py:37
  82.1 86.9 %while.15 = (s32[]{:T(128)}, f32[4]{0:T(128)S(1)}, f32[4]{0:T(128)S(1)}, bf16[4,384,768]{2,1,0:T(8,128)(2,1)}, f32[4,384]{1,0:T(4,128)S(1)}, /*index=5*/bf16[4,7...) while((s32[]{:T(128)}, f32[4]{0:T(128)S(1)}, ...), condition=%wide.region_6.8_spmd.clone, body=%wide.region_0.7_spmd.clone.sunk | while | flops 4096644864 | bytes 44915888 | solution.py:76
  82.9 7.9 %fusion.72 = (f32[384]{0:T(512)S(1)}, f32[384,3072]{1,0:T(8,128)}) fusion(bf16[3072,768]{1,0:T(8,128)(2,1)} %get-tuple-element.241, bf16[384,768]{1,0:T(8,128)(2,1)} %get-tuple-element.240, bf16[4,768,768]{2,1,0:T(8,128)(2,1)} %get-tuple-element.239, s32[]{:T(128)} %get-tuple-element.223, pred[3072]{0:T(1024)(128)(4,1)S(1)} %fusion.71), kind=kOutput, calls=%fused_computation.58.clone.1 | convolution fusion | flops 2268757504 | bytes 11211776 | tf_op jit(solution)/shard_map/while/body/eval_jaxpr/dot_general | solution.py:52
  90.8 4.1 %fusion.73 = (f32[384]{0:T(512)S(1)}, f32[384]{0:T(512)S(1)}) fusion(f32[384,3072]{1,0:T(8,128)} %get-tuple-element.205, s32[384]{0:T(512)S(1)} %dynamic-slice_reduce_fusion.2, f32[384]{0:T(512)S(1)} %get-tuple-element.206, pred[3072]{0:T(1024)(128)(4,1)S(1)} %fusion.71), kind=kLoop, calls=%fused_computation.7.clone.1 | loop fusion | flops 7077120 | bytes 4727808 | tf_op jit(solution)/shard_map/while/body/eval_jaxpr/reduce_sum | solution.py:64
  96.3 6.0 %fusion.74 = bf16[4,384,768]{2,1,0:T(8,128)(2,1)} fusion(bf16[4,384,768]{2,1,0:T(8,128)(2,1)} %get-tuple-element.226, s32[]{:T(128)} %get-tuple-element.223, bf16[3072,768]{1,0:T(8,128)(2,1)} %get-tuple-element.241, f32[384,3072]{1,0:T(8,128)S(1)} %copy-done.1, f32[384]{0:T(512)S(1)} %get-tuple-element.211, f32[384]{0:T(512)S(1)} %get-tuple-element.204, ...), kind=kOutput, calls=%fused_computation.23.clone.1 | convolution fusion | flops 1820786688 | bytes 10035200 | tf_op jit(solution)/shard_map/while/body/eval_jaxpr/dot_general | solution.py:71
  104.6 7.9 %fusion.72 = (f32[384]{0:T(512)S(1)}, f32[384,3072]{1,0:T(8,128)}) fusion(bf16[3072,768]{1,0:T(8,128)(2,1)} %get-tuple-element.241, bf16[384,768]{1,0:T(8,128)(2,1)} %get-tuple-element.240, bf16[4,768,768]{2,1,0:T(8,128)(2,1)} %get-tuple-element.239, s32[]{:T(128)} %get-tuple-element.223, pred[3072]{0:T(1024)(128)(4,1)S(1)} %fusion.71), kind=kOutput, calls=%fused_computation.58.clone.1 | convolution fusion | flops 2268757504 | bytes 11211776 | tf_op jit(solution)/shard_map/while/body/eval_jaxpr/dot_general | solution.py:52
  112.6 4.1 %fusion.73 = (f32[384]{0:T(512)S(1)}, f32[384]{0:T(512)S(1)}) fusion(f32[384,3072]{1,0:T(8,128)} %get-tuple-element.205, s32[384]{0:T(512)S(1)} %dynamic-slice_reduce_fusion.2, f32[384]{0:T(512)S(1)} %get-tuple-element.206, pred[3072]{0:T(1024)(128)(4,1)S(1)} %fusion.71), kind=kLoop, calls=%fused_computation.7.clone.1 | loop fusion | flops 7077120 | bytes 4727808 | tf_op jit(solution)/shard_map/while/body/eval_jaxpr/reduce_sum | solution.py:64
  118.0 6.0 %fusion.74 = bf16[4,384,768]{2,1,0:T(8,128)(2,1)} fusion(bf16[4,384,768]{2,1,0:T(8,128)(2,1)} %get-tuple-element.226, s32[]{:T(128)} %get-tuple-element.223, bf16[3072,768]{1,0:T(8,128)(2,1)} %get-tuple-element.241, f32[384,3072]{1,0:T(8,128)S(1)} %copy-done.1, f32[384]{0:T(512)S(1)} %get-tuple-element.211, f32[384]{0:T(512)S(1)} %get-tuple-element.204, ...), kind=kOutput, calls=%fused_computation.23.clone.1 | convolution fusion | flops 1820786688 | bytes 10035200 | tf_op jit(solution)/shard_map/while/body/eval_jaxpr/dot_general | solution.py:71
  126.4 7.9 %fusion.72 = (f32[384]{0:T(512)S(1)}, f32[384,3072]{1,0:T(8,128)}) fusion(bf16[3072,768]{1,0:T(8,128)(2,1)} %get-tuple-element.241, bf16[384,768]{1,0:T(8,128)(2,1)} %get-tuple-element.240, bf16[4,768,768]{2,1,0:T(8,128)(2,1)} %get-tuple-element.239, s32[]{:T(128)} %get-tuple-element.223, pred[3072]{0:T(1024)(128)(4,1)S(1)} %fusion.71), kind=kOutput, calls=%fused_computation.58.clone.1 | convolution fusion | flops 2268757504 | bytes 11211776 | tf_op jit(solution)/shard_map/while/body/eval_jaxpr/dot_general | solution.py:52
  134.3 4.1 %fusion.73 = (f32[384]{0:T(512)S(1)}, f32[384]{0:T(512)S(1)}) fusion(f32[384,3072]{1,0:T(8,128)} %get-tuple-element.205, s32[384]{0:T(512)S(1)} %dynamic-slice_reduce_fusion.2, f32[384]{0:T(512)S(1)} %get-tuple-element.206, pred[3072]{0:T(1024)(128)(4,1)S(1)} %fusion.71), kind=kLoop, calls=%fused_computation.7.clone.1 | loop fusion | flops 7077120 | bytes 4727808 | tf_op jit(solution)/shard_map/while/body/eval_jaxpr/reduce_sum | solution.py:64
  139.7 6.1 %fusion.74 = bf16[4,384,768]{2,1,0:T(8,128)(2,1)} fusion(bf16[4,384,768]{2,1,0:T(8,128)(2,1)} %get-tuple-element.226, s32[]{:T(128)} %get-tuple-element.223, bf16[3072,768]{1,0:T(8,128)(2,1)} %get-tuple-element.241, f32[384,3072]{1,0:T(8,128)S(1)} %copy-done.1, f32[384]{0:T(512)S(1)} %get-tuple-element.211, f32[384]{0:T(512)S(1)} %get-tuple-element.204, ...), kind=kOutput, calls=%fused_computation.23.clone.1 | convolution fusion | flops 1820786688 | bytes 10035200 | tf_op jit(solution)/shard_map/while/body/eval_jaxpr/dot_general | solution.py:71
  148.1 7.9 %fusion.72 = (f32[384]{0:T(512)S(1)}, f32[384,3072]{1,0:T(8,128)}) fusion(bf16[3072,768]{1,0:T(8,128)(2,1)} %get-tuple-element.241, bf16[384,768]{1,0:T(8,128)(2,1)} %get-tuple-element.240, bf16[4,768,768]{2,1,0:T(8,128)(2,1)} %get-tuple-element.239, s32[]{:T(128)} %get-tuple-element.223, pred[3072]{0:T(1024)(128)(4,1)S(1)} %fusion.71), kind=kOutput, calls=%fused_computation.58.clone.1 | convolution fusion | flops 2268757504 | bytes 11211776 | tf_op jit(solution)/shard_map/while/body/eval_jaxpr/dot_general | solution.py:52
  156.0 4.1 %fusion.73 = (f32[384]{0:T(512)S(1)}, f32[384]{0:T(512)S(1)}) fusion(f32[384,3072]{1,0:T(8,128)} %get-tuple-element.205, s32[384]{0:T(512)S(1)} %dynamic-slice_reduce_fusion.2, f32[384]{0:T(512)S(1)} %get-tuple-element.206, pred[3072]{0:T(1024)(128)(4,1)S(1)} %fusion.71), kind=kLoop, calls=%fused_computation.7.clone.1 | loop fusion | flops 7077120 | bytes 4727808 | tf_op jit(solution)/shard_map/while/body/eval_jaxpr/reduce_sum | solution.py:64
  161.4 6.1 %fusion.74 = bf16[4,384,768]{2,1,0:T(8,128)(2,1)} fusion(bf16[4,384,768]{2,1,0:T(8,128)(2,1)} %get-tuple-element.226, s32[]{:T(128)} %get-tuple-element.223, bf16[3072,768]{1,0:T(8,128)(2,1)} %get-tuple-element.241, f32[384,3072]{1,0:T(8,128)S(1)} %copy-done.1, f32[384]{0:T(512)S(1)} %get-tuple-element.211, f32[384]{0:T(512)S(1)} %get-tuple-element.204, ...), kind=kOutput, calls=%fused_computation.23.clone.1 | convolution fusion | flops 1820786688 | bytes 10035200 | tf_op jit(solution)/shard_map/while/body/eval_jaxpr/dot_general | solution.py:71
  169.0 8.1 %fusion.42 = f32[768,4,768]{2,0,1:T(8,128)} fusion(bf16[4,384,768]{2,1,0:T(8,128)(2,1)} %get-tuple-element.64, bf16[384,768]{1,0:T(8,128)(2,1)} %get-tuple-element.249), kind=kOutput, calls=%fused_computation.40 | convolution fusion | flops 1811939328 | bytes 12386304 | tf_op jit(solution)/shard_map/nd,tne->dte/dot_general | solution.py:83
  183.1 7.4 %all-reduce.10 = (f32[4]{0:T(128)S(1)}, f32[4]{0:T(128)S(1)}) all-reduce(f32[4]{0:T(128)S(1)} %dynamic-update-slice, f32[4]{0:T(128)S(1)} %dynamic-update-slice.4), channel_id=1, replica_groups=mesh['don_0'=4,'don_1'=2,'acc_0'=4,'acc_1'=4] {'don_0'}, use_global_device_ids=true, to_apply=%add | all-reduce | flops 8 | bytes 64
  195.2 4.0 %all-reduce.11 = (f32[2]{0:T(128)S(1)}, f32[2]{0:T(128)S(1)}) all-reduce(f32[2]{0:T(128)S(1)} %dynamic-update-slice.1, f32[2]{0:T(128)S(1)} %dynamic-update-slice.5), channel_id=1, replica_groups=mesh['don_0'=4,'don_1'=2,'acc_0'=4,'acc_1'=4] {'don_1'}, use_global_device_ids=true, to_apply=%add.1 | all-reduce | flops 4 | bytes 32
  203.9 8.7 %all-reduce.9 = (f32[4]{0:T(128)S(1)}, f32[4]{0:T(128)S(1)}) all-reduce(f32[4]{0:T(128)S(1)} %dynamic-update-slice.2, f32[4]{0:T(128)S(1)} %dynamic-update-slice.6), channel_id=1, replica_groups=mesh['don_0'=4,'don_1'=2,'acc_0'=4,'acc_1'=4] {'acc_0'}, use_global_device_ids=true, to_apply=%add.2 | all-reduce | flops 8 | bytes 64
  213.9 1.4 dynamic-update-slice.7
  216.8 7.4 %all-reduce.8 = (f32[4]{0:T(128)S(1)}, f32[4]{0:T(128)S(1)}) all-reduce(f32[4]{0:T(128)S(1)} %dynamic-update-slice.3, f32[4]{0:T(128)S(1)} %dynamic-update-slice.7), channel_id=1, replica_groups=mesh['don_0'=4,'don_1'=2,'acc_0'=4,'acc_1'=4] {'acc_1'}, use_global_device_ids=true, to_apply=%add.3 | all-reduce | flops 8 | bytes 64
  226.7 4.8 %reduce-scatter.2.cloned.1.call-done = f32[96,4,768]{2,0,1:T(8,128)} async-done(((f32[768,4,768]{2,0,1:T(8,128)}), f32[96,4,768]{2,0,1:T(8,128)}) %reduce-scatter.2.cloned.1.call-update) | async-done | bytes 1179664 | tf_op jit(solution)/shard_map/reduce_scatter | solution.py:82
  231.5 3.0 %copy.12 = f32[96,4,768]{2,1,0:T(4,128)} copy(f32[96,4,768]{2,0,1:T(8,128)} %reduce-scatter.2.cloned.1.call-done) | data formatting | bytes 2359296
  (97 shorter events, 38.7 us)
Async XLA Ops:
  7.2 1.9 copy-start
  7.2 74.9 %all-gather.2.cloned.1.call-start = ((), (), s32[]{:S(2)}) async-start(), calls=%async_computation.1 | async-start | bytes 4755456 | tf_op jit(solution)/shard_map/all_gather | solution.py:37
  10.4 221.1 %reduce-scatter.2.cloned.1.call-start = ((), (), s32[]{:S(2)}) async-start(), calls=%async_computation.2 | async-start | bytes 10616832 | tf_op jit(solution)/shard_map/reduce_scatter | solution.py:82
  90.8 5.5 %copy-start.1 = (f32[384,3072]{1,0:T(8,128)S(1)}, f32[384,3072]{1,0:T(8,128)}, u32[]{:S(2)}) copy-start(f32[384,3072]{1,0:T(8,128)} %get-tuple-element.205) | copy-start | bytes 14155780 | tf_op jit(solution)/shard_map/while
  112.5 5.5 %copy-start.1 = (f32[384,3072]{1,0:T(8,128)S(1)}, f32[384,3072]{1,0:T(8,128)}, u32[]{:S(2)}) copy-start(f32[384,3072]{1,0:T(8,128)} %get-tuple-element.205) | copy-start | bytes 14155780 | tf_op jit(solution)/shard_map/while
  134.2 5.5 %copy-start.1 = (f32[384,3072]{1,0:T(8,128)S(1)}, f32[384,3072]{1,0:T(8,128)}, u32[]{:S(2)}) copy-start(f32[384,3072]{1,0:T(8,128)} %get-tuple-element.205) | copy-start | bytes 14155780 | tf_op jit(solution)/shard_map/while
  156.0 5.5 %copy-start.1 = (f32[384,3072]{1,0:T(8,128)S(1)}, f32[384,3072]{1,0:T(8,128)}, u32[]{:S(2)}) copy-start(f32[384,3072]{1,0:T(8,128)} %get-tuple-element.205) | copy-start | bytes 14155780 | tf_op jit(solution)/shard_map/while
  177.1 0.7 copy-start.5
  177.1 5.4 %copy-start.4 = (u32[128]{0:T(128)S(1)}, u32[128]{0:T(128)}, u32[]{:S(2)}) copy-start(u32[128]{0:T(128)} %constant.79) | copy-start | bytes 1540
  177.1 17.5 %copy-start.3 = (u32[128]{0:T(128)S(1)}, u32[128]{0:T(128)}, u32[]{:S(2)}) copy-start(u32[128]{0:T(128)} %constant.84) | copy-start | bytes 1540
  177.1 26.2 %copy-start.2 = (u32[128]{0:T(128)S(1)}, u32[128]{0:T(128)}, u32[]{:S(2)}) copy-start(u32[128]{0:T(128)} %constant.89) | copy-start | bytes 1540
Sparse Core Ops, SparseCore 0:
  11.7 70.3 all-gather.1
  177.3 54.2 reduce-scatter.1
